TPU v7x, 32 devices: a whole 2x2x4 slice. The times are simulated.
32 devices in a mesh: rep: 8 (over y, x, core), tp: 4 (over z).
Axes of the slice: x: 2, y: 2, z: 4, core: 2. Of those that a mesh axis runs over, the one named last changes fastest.
Arguments:
- hidden: bfloat16 [512, 8192], P('rep'), may hold values from -6 to 6
- norm_gain: bfloat16 [8192], replicated, may hold values from 0.5 to 1.5
- query_weight_matrix: bfloat16 [8192, 4096], P(None, 'tp'), may hold values from -0.0625 to 0.0625
- key_value_weight: bfloat16 [2, 8192, 1024], P(None, None, 'tp'), may hold values from -0.0625 to 0.0625
- output_weight_matrix: bfloat16 [4096, 8192], P('tp'), may hold values from -0.375 to 0.375
- input_down_factors: bfloat16 [3, 8192, 64], P(None, ('rep', 'tp')), may hold values from -0.0625 to 0.0625
- query_up_factor: bfloat16 [64, 4096], P(None, ('rep', 'tp')), may hold values from -0.75 to 0.75
- key_value_up_factors: bfloat16 [2, 64, 1024], P(None, None, ('rep', 'tp')), may hold values from -0.75 to 0.75
- output_down_factor: bfloat16 [4096, 64], P(('rep', 'tp')), may hold values from -0.375 to 0.375
- output_up_factor: bfloat16 [64, 8192], P(None, ('rep', 'tp')), may hold values from -0.75 to 0.75
- cache_keys: bfloat16 [512, 8, 128, 128], P('rep', 'tp'), may hold values from -360 to 360
- cache_values: bfloat16 [512, 8, 128, 128], P('rep', 'tp'), may hold values from -6 to 6
- lengths: int32 [512], P('rep'), may hold values from 1 to 127
Outputs:
- attn_out: bfloat16 [512, 8192], P('rep', 'tp')
All inputs are finite; a program needn't handle non-finite values.
Results may differ from a plain program's by a relative error of at most 0.03.
Values may be sent and summed in bfloat16 or wider, within the bound.
A program may use at most 128 MiB of HBM per device.

v0:
```python
import math
import jax
import jax.numpy as jnp
from jax import lax
from jax.sharding import PartitionSpec as P

epsilon = 1e-06
rope_base = 1000000.0
adapter_scale = 0.5


def rope_angles(lengths, head_dim):
    half_dim = head_dim // 2
    frequency = rope_base ** (-(jnp.arange(half_dim, dtype=jnp.float32) * 2.0) / head_dim)
    return lengths.astype(jnp.float32)[:, None] * frequency[None, :]


def rotate(vectors, angles):
    half_dim = vectors.shape[-1] // 2
    cosine = jnp.cos(angles)[:, None, :]
    sine_part = jnp.sin(angles)[:, None, :]
    low_half = vectors[..., :half_dim]
    high_half = vectors[..., half_dim:]
    return jnp.concatenate(
        [low_half * cosine - high_half * sine_part, high_half * cosine + low_half * sine_part],
        axis=-1,
    )


def adapted(normed, frozen_matrix, inner_part, up_factor):
    base_part = jnp.dot(normed, frozen_matrix, preferred_element_type=jnp.float32)
    return base_part + adapter_scale * jnp.dot(
        inner_part, up_factor, preferred_element_type=jnp.float32
    )


def attend(query, new_key, new_value, keys, values, lengths):
    score_scale = 1.0 / math.sqrt(keys.shape[-1])
    scores = (
        jnp.einsum(
            "bkgd,bkld->bkgl", query, keys.astype(jnp.float32), precision=lax.Precision.HIGHEST
        )
        * score_scale
    )
    own_score = jnp.sum(query * new_key.astype(jnp.float32)[:, :, None, :], axis=-1) * score_scale
    live_mask = (
        jnp.arange(keys.shape[2], dtype=jnp.int32)[None, None, None, :]
        < lengths[:, None, None, None]
    )
    row_max = jnp.maximum(jnp.max(jnp.where(live_mask, scores, -1e30), axis=-1), own_score)
    weights = jnp.where(live_mask, jnp.exp(scores - row_max[..., None]), 0.0)
    own_weight = jnp.exp(own_score - row_max)
    denom_sum = jnp.sum(weights, axis=-1) + own_weight
    probs = (weights / denom_sum[..., None]).astype(jnp.bfloat16)
    own_prob = (own_weight / denom_sum).astype(jnp.bfloat16)
    context = jnp.einsum("bkgl,bkld->bkgd", probs, values, preferred_element_type=jnp.float32)
    context = (
        context
        + own_prob.astype(jnp.float32)[..., None] * new_value.astype(jnp.float32)[:, :, None, :]
    )
    return context.astype(jnp.bfloat16)


def regroup(factor, tp_count, group):
    count, rank_dim, wide = factor.shape
    return factor.reshape(count, rank_dim, tp_count, group, wide // (tp_count * group))


def settle(factor):
    count, rank_dim, tp_count, group, piece = factor.shape
    return jnp.swapaxes(factor, 2, 3).reshape(count, rank_dim, group * tp_count * piece)


def local(
    hidden,
    norm_gain,
    query_weight_matrix,
    key_value_weight,
    output_weight_matrix,
    input_down_factors,
    query_up_factor,
    key_value_up_factors,
    output_down_factor,
    output_up_factor,
    cache_keys,
    cache_values,
    lengths,
):
    states = hidden.astype(jnp.float32)
    square = jnp.mean(states * states, axis=-1, keepdims=True)
    normed = (states * lax.rsqrt(square + epsilon) * norm_gain.astype(jnp.float32)).astype(
        jnp.bfloat16
    )
    seq_count = hidden.shape[0]
    block_rows = input_down_factors.shape[1]
    rep_count = lax.axis_size("rep")
    tp_count = lax.axis_size("tp")
    tp_index = lax.axis_index("tp")
    own_features = lax.dynamic_slice_in_dim(
        normed.reshape(seq_count, rep_count, tp_count, block_rows), tp_index, 1, 2
    )
    own_features = own_features.reshape(seq_count, rep_count * block_rows)
    partial_inner = jnp.einsum(
        "bd,jdr->jbr",
        own_features,
        lax.all_gather(input_down_factors, "rep", axis=1, tiled=True),
        preferred_element_type=jnp.float32,
    )
    inner = lax.psum(partial_inner.astype(jnp.bfloat16), "tp")
    query_up_rows = query_up_factor[None]
    out_down_rows = jnp.swapaxes(output_down_factor, 0, 1)[None]
    out_up_rows = output_up_factor[None]
    per_rep = (
        lax.all_gather(query_up_rows, "rep", axis=2, tiled=True),
        lax.all_gather(key_value_up_factors, "rep", axis=2, tiled=True),
        lax.all_gather(out_down_rows, "rep", axis=2, tiled=True),
        lax.all_gather(out_up_rows, "rep", axis=2, tiled=True),
    )
    group = rep_count // tp_count
    arrived = (
        lax.all_to_all(
            regroup(per_rep[0], tp_count, group), "tp", split_axis=2, concat_axis=2, tiled=True
        ),
        lax.all_to_all(
            regroup(per_rep[1], tp_count, group), "tp", split_axis=2, concat_axis=2, tiled=True
        ),
        lax.all_to_all(
            regroup(per_rep[2], tp_count, group), "tp", split_axis=2, concat_axis=2, tiled=True
        ),
        lax.all_to_all(
            regroup(per_rep[3], tp_count, group), "tp", split_axis=2, concat_axis=2, tiled=True
        ),
    )
    query_up_local = settle(arrived[0])
    key_value_up_local = settle(arrived[1])
    out_down_local = settle(arrived[2])
    out_up_local = settle(arrived[3])
    kv_local = cache_keys.shape[1]
    head_dim = cache_keys.shape[3]
    angles = rope_angles(lengths, head_dim)
    query = adapted(normed, query_weight_matrix, inner[0], query_up_local[0]).reshape(
        seq_count, -1, head_dim
    )
    query = rotate(query, angles).reshape(seq_count, kv_local, -1, head_dim)
    new_key = adapted(normed, key_value_weight[0], inner[1], key_value_up_local[0]).reshape(
        seq_count, kv_local, head_dim
    )
    new_key = rotate(new_key, angles).astype(jnp.bfloat16)
    new_value = (
        adapted(normed, key_value_weight[1], inner[2], key_value_up_local[1])
        .reshape(seq_count, kv_local, head_dim)
        .astype(jnp.bfloat16)
    )
    context = attend(query, new_key, new_value, cache_keys, cache_values, lengths).reshape(
        seq_count, -1
    )
    partial_middle = jnp.einsum(
        "bh,rh->br", context, out_down_local[0], preferred_element_type=jnp.float32
    )
    middle = lax.psum(partial_middle, "tp").astype(jnp.bfloat16)
    partial_value = jnp.dot(context, output_weight_matrix, preferred_element_type=jnp.float32)
    summed = lax.psum_scatter(
        partial_value.astype(jnp.bfloat16), "tp", scatter_dimension=1, tiled=True
    ).astype(jnp.float32)
    summed = summed + adapter_scale * jnp.dot(
        middle, out_up_local[0], preferred_element_type=jnp.float32
    )
    return summed.astype(jnp.bfloat16)


def solution(mesh):
    return jax.shard_map(
        local,
        mesh=mesh,
        in_specs=(
            P("rep", None),
            P(),
            P(None, "tp"),
            P(None, None, "tp"),
            P("tp", None),
            P(None, ("rep", "tp"), None),
            P(None, ("rep", "tp")),
            P(None, None, ("rep", "tp")),
            P(("rep", "tp"), None),
            P(None, ("rep", "tp")),
            P("rep", "tp", None, None),
            P("rep", "tp", None, None),
            P("rep"),
        ),
        out_specs=P("rep", "tp"),
        check_vma=False,
    )
```

profile of v0, /device:TPU:0, one launch (start us, length us, event | category | flops | bytes accessed | tf_op | source)
XLA Modules:
  0.0 177.4 jit_solution(7634904349694602952)
XLA Ops:
  6.5 10.9 %all_gather.17 = bf16[2,64,256]{1,2,0:T(8,128)(2,1)S(1)} all-gather(bf16[2,64,32]{1,2,0:T(8,128)(2,1)} %param.20), channel_id=1, replica_groups=mesh['rep'=8,'tp'=4] {'rep'}, dimensions={2}, use_global_device_ids=true | all-gather | bytes 73728 | tf_op jit(solution)/shard_map/all_gather | solution.py:115
  17.4 0.8 reshape.203
  18.2 4.9 %all-to-all-start.1 = ((bf16[4,2,4096]{2,1,0:T(2,128)(2,1)}), bf16[4,2,4096]{2,1,0:T(2,128)(2,1)S(1)}, u32[]{:S(2)}, u32[]{:S(2)}) async-start(bf16[4,2,4096]{2,1,0:T(2,128)(2,1)} %reshape.203), calls=%async_computation.1 | async-start | bytes 131072 | tf_op jit(solution)/shard_map/all_to_all | solution.py:124
  23.1 0.7 convert_element_type.82
  23.8 1.5 fusion.8
  25.4 1.5 fusion.10
  26.9 0.8 reshape.182
  27.7 3.0 %fusion.2 = f32[64,256]{1,0:T(8,128)S(1)} fusion(bf16[64,8192]{1,0:T(8,128)(2,1)S(1)} %fusion.10, bf16[2,8192,256]{2,1,0:T(8,128)(2,1)} %param.16), kind=kOutput, calls=%fused_computation.3 | convolution fusion | flops 268435456 | bytes 5308416 | tf_op jit(solution)/shard_map/dot_general | solution.py:31
  30.7 3.0 %fusion = f32[64,256]{1,0:T(8,128)S(1)} fusion(bf16[64,8192]{1,0:T(8,128)(2,1)S(1)} %fusion.10, bf16[2,8192,256]{2,1,0:T(8,128)(2,1)} %param.16), kind=kOutput, calls=%fused_computation.1 | convolution fusion | flops 268435456 | bytes 5308416 | tf_op jit(solution)/shard_map/dot_general | solution.py:31
  33.8 1.5 dynamic-slice_reduce_fusion
  35.3 0.1 reshape.199
  35.5 12.6 %all_gather.15 = bf16[3,2048,64]{1,2,0:T(8,128)(2,1)S(1)} all-gather(bf16[3,256,64]{1,2,0:T(8,128)(2,1)S(1)} %copy-done), channel_id=1, replica_groups=mesh['rep'=8,'tp'=4] {'rep'}, dimensions={1}, use_global_device_ids=true | all-gather | bytes 884736 | tf_op jit(solution)/shard_map/all_gather | solution.py:106
  48.0 0.4 fusion.17
  48.5 0.2 multiply_cosine_fusion
  48.8 8.3 %all-gather = bf16[64,1024]{1,0:T(8,128)(2,1)S(1)} all-gather(bf16[64,128]{1,0:T(8,128)(2,1)S(1)} %copy-done.2), channel_id=2, replica_groups=mesh['rep'=8,'tp'=4] {'rep'}, dimensions={1}, use_global_device_ids=true | all-gather | bytes 147456 | tf_op jit(solution)/shard_map/all_gather | solution.py:114
  57.1 0.7 copy.50
  57.9 19.8 %psum.14 = bf16[3,64,64]{2,1,0:T(8,128)(2,1)S(1)} all-reduce(bf16[3,64,64]{2,1,0:T(8,128)(2,1)S(1)} %fusion.17), channel_id=1, replica_groups=mesh['rep'=8,'tp'=4] {'tp'}, use_global_device_ids=true, to_apply=%region_1.0 | all-reduce | flops 12288 | bytes 49152 | tf_op jit(solution)/shard_map/psum | solution.py:109
  77.7 3.3 %all-to-all-start = ((bf16[1,64,4,2,128]{4,3,1,0,2:T(2,128)(2,1)}), bf16[1,64,4,2,128]{4,3,1,0,2:T(2,128)(2,1)S(1)}, u32[]{:S(2)}, u32[]{:S(2)}) async-start(bf16[1,64,4,2,128]{4,3,1,0,2:T(2,128)(2,1)} %copy.50), calls=%async_computation | async-start | bytes 262144 | tf_op jit(solution)/shard_map/all_to_all | solution.py:121
  81.1 0.2 reduce-scatter.2.cloned.1.call-start
  81.3 0.1 reshape.204
  81.5 0.2 fusion.14
  81.7 0.2 fusion.16
  81.9 0.2 subtract_convert_fusion
  82.2 4.7 %all-to-all-done = bf16[1,64,4,2,128]{4,3,1,0,2:T(2,128)(2,1)S(1)} async-done(((bf16[1,64,4,2,128]{4,3,1,0,2:T(2,128)(2,1)}), bf16[1,64,4,2,128]{4,3,1,0,2:T(2,128)(2,1)S(1)}, u32[]{:S(2)}, u32[]{:S(2)}) %all-to-all-start) | async-done | bytes 131104 | tf_op jit(solution)/shard_map/all_to_all | solution.py:121
  86.9 0.2 copy.51
  87.2 0.2 convolution_multiply_fusion.2
  87.4 8.8 %fusion.11 = f32[8,8,8,128]{3,1,2,0:T(8,128)S(1)} fusion(f32[64,1024]{1,0:T(8,128)S(1)} %convolution_multiply_fusion.2, bf16[64,8192]{1,0:T(8,128)(2,1)S(1)} %fusion.10, bf16[8192,1024]{1,0:T(8,128)(2,1)} %param.15), kind=kOutput, calls=%fused_computation.19 | convolution fusion | flops 1073807360 | bytes 18350080 | tf_op jit(solution)/shard_map/dot_general | solution.py:31
  96.2 0.2 multiply_subtract_fusion
  96.4 0.1 pad_maximum_fusion
  96.6 0.4 fusion.18
  97.1 8.5 %select_reduce_fusion = (f32[64,2,4]{2,1,0:T(2,128)S(1)}, f32[64,2,4,128]{3,2,1,0:T(4,128)S(1)}) fusion(pred[64,128]{1,0:T(8,128)(4,1)S(1)} %iota_compare_fusion, f32[64,2,4,128]{3,2,1,0:T(4,128)S(1)} %bitcast.58, bf16[64,2,128,128]{3,2,1,0:T(8,128)(2,1)} %param.23), kind=kOutput, calls=%fused_computation.34 | convolution fusion | flops 100859392 | bytes 4728832 | tf_op jit(solution)/shard_map/bkgd,bkld->bkgl/dot_general | solution.py:40
  105.7 0.1 copy.56
  105.8 0.4 fusion.19
  106.6 3.5 %fusion.12 = bf16[64,2,4,128]{3,2,1,0:T(4,128)(2,1)S(1)} fusion(bf16[64,2,128,128]{3,2,1,0:T(8,128)(2,1)} %param.24, f32[64,2,4,128]{3,2,1,0:T(4,128)S(1)} %get-tuple-element.16, f32[64,2,128]{2,1,0:T(2,128)S(1)} %reshape.192, f32[64,2,4]{2,1,0:T(2,128)S(1)} %copy.59, f32[64,2,4]{2,1,0:T(2,128)S(1)} %copy.58, f32[64,2,4]{2,1,0:T(2,128)S(1)} %copy.56, ...), kind=kOutput, calls=%fused_computation.20 | convolution fusion | flops 17235968 | bytes 4667392 | tf_op jit(solution)/shard_map/bkgl,bkld->bkgd/dot_general | solution.py:56
  110.2 9.8 %convolution_convert_fusion = bf16[64,8192]{1,0:T(8,128)(2,1)} fusion(bf16[64,1024]{1,0:T(8,128)(2,1)S(1)} %reshape.189, bf16[1024,8192]{1,0:T(8,128)(2,1)} %param.17), kind=kOutput, calls=%fused_computation | convolution fusion | flops 1074266112 | bytes 17956864 | tf_op jit(solution)/shard_map/dot_general | solution.py:161
  120.0 8.2 %all-gather.1 = bf16[64,1024]{1,0:T(8,128)(2,1)S(1)} all-gather(bf16[64,128]{1,0:T(8,128)(2,1)S(1)} %bitcast.66), channel_id=3, replica_groups=mesh['rep'=8,'tp'=4] {'rep'}, dimensions={1}, use_global_device_ids=true | all-gather | bytes 147456 | tf_op jit(solution)/shard_map/all_gather | solution.py:116
  128.2 0.7 copy.61
  129.0 3.3 %all-to-all-start.2 = ((bf16[1,64,4,2,128]{4,3,1,0,2:T(2,128)(2,1)}), bf16[1,64,4,2,128]{4,3,1,0,2:T(2,128)(2,1)S(1)}, u32[]{:S(2)}, u32[]{:S(2)}) async-start(bf16[1,64,4,2,128]{4,3,1,0,2:T(2,128)(2,1)} %copy.61), calls=%async_computation.3 | async-start | bytes 262144 | tf_op jit(solution)/shard_map/all_to_all | solution.py:127
  132.3 9.8 %all-gather.2 = bf16[64,2048]{1,0:T(8,128)(2,1)S(1)} all-gather(bf16[64,256]{1,0:T(8,128)(2,1)S(1)} %copy-done.1), channel_id=4, replica_groups=mesh['rep'=8,'tp'=4] {'rep'}, dimensions={1}, use_global_device_ids=true | all-gather | bytes 294912 | tf_op jit(solution)/shard_map/all_gather | solution.py:117
  142.1 0.2 reshape.191
  142.2 0.9 copy.63
  143.1 5.0 %all-to-all-start.3 = ((bf16[1,64,4,2,256]{4,3,1,0,2:T(2,128)(2,1)}), bf16[1,64,4,2,256]{4,3,1,0,2:T(2,128)(2,1)S(1)}, u32[]{:S(2)}, u32[]{:S(2)}) async-start(bf16[1,64,4,2,256]{4,3,1,0,2:T(2,128)(2,1)} %copy.63), calls=%async_computation.4 | async-start | bytes 524288 | tf_op jit(solution)/shard_map/all_to_all | solution.py:130
  148.2 0.2 copy.62
  148.4 0.2 fusion.29
  148.6 19.5 %psum.15 = bf16[64,64]{1,0:T(8,128)(2,1)S(1)} all-reduce(f32[64,64]{1,0:T(8,128)S(1)} %fusion.29), channel_id=1, replica_groups=mesh['rep'=8,'tp'=4] {'tp'}, use_global_device_ids=true, to_apply=%region_6.7 | all-reduce | flops 4096 | bytes 24576 | tf_op jit(solution)/shard_map/psum | solution.py:160
  168.1 0.3 copy.64
  168.5 0.2 squeeze_reshape.11
  168.7 1.9 %fusion.7 = bf16[64,2048]{1,0:T(8,128)(2,1)} fusion(bf16[64,2048]{1,0:T(8,128)(2,1)S(1)} %squeeze_reshape.11, bf16[64,2048]{1,0:T(8,128)(2,1)} %reduce-scatter.2.cloned.1.call-done, bf16[64,64]{1,0:T(8,128)(2,1)S(1)} %psum.15), kind=kOutput, calls=%fused_computation.11 | convolution fusion | flops 17301504 | bytes 794624 | tf_op jit(solution)/shard_map/dot_general | solution.py:165
  (40 shorter events, 1.3 us)
Async XLA Ops:
  18.2 59.5 %all-to-all-start.1 = ((bf16[4,2,4096]{2,1,0:T(2,128)(2,1)}), bf16[4,2,4096]{2,1,0:T(2,128)(2,1)S(1)}, u32[]{:S(2)}, u32[]{:S(2)}) async-start(bf16[4,2,4096]{2,1,0:T(2,128)(2,1)} %reshape.203), calls=%async_computation.1 | async-start | bytes 131072 | tf_op jit(solution)/shard_map/all_to_all | solution.py:124
  30.7 4.7 %copy-start = (bf16[3,256,64]{1,2,0:T(8,128)(2,1)S(1)}, bf16[3,256,64]{1,2,0:T(8,128)(2,1)}, u32[]{:S(2)}) copy-start(bf16[3,256,64]{1,2,0:T(8,128)(2,1)} %param.18) | copy-start | bytes 294916
  30.7 17.3 %copy-start.4 = (s32[64]{0:T(128)S(1)}, s32[64]{0:T(128)}, u32[]{:S(2)}) copy-start(s32[64]{0:T(128)} %param.25) | copy-start | bytes 772
  30.7 18.0 %copy-start.2 = (bf16[64,128]{1,0:T(8,128)(2,1)S(1)}, bf16[64,128]{1,0:T(8,128)(2,1)}, u32[]{:S(2)}) copy-start(bf16[64,128]{1,0:T(8,128)(2,1)} %param.19) | copy-start | bytes 49156
  77.7 9.2 %all-to-all-start = ((bf16[1,64,4,2,128]{4,3,1,0,2:T(2,128)(2,1)}), bf16[1,64,4,2,128]{4,3,1,0,2:T(2,128)(2,1)S(1)}, u32[]{:S(2)}, u32[]{:S(2)}) async-start(bf16[1,64,4,2,128]{4,3,1,0,2:T(2,128)(2,1)} %copy.50), calls=%async_computation | async-start | bytes 262144 | tf_op jit(solution)/shard_map/all_to_all | solution.py:121
  81.1 87.6 %reduce-scatter.2.cloned.1.call-start = ((), (), s32[]{:S(2)}) async-start(), calls=%async_computation.5 | async-start | bytes 1310720 | tf_op jit(solution)/shard_map/reduce_scatter | solution.py:162
  110.2 9.8 %copy-start.3 = (bf16[128,64]{0,1:T(8,128)(2,1)S(1)}, bf16[128,64]{0,1:T(8,128)(2,1)}, u32[]{:S(2)}) copy-start(bf16[128,64]{0,1:T(8,128)(2,1)} %param.21) | copy-start | bytes 49156
  110.2 22.1 %copy-start.1 = (bf16[64,256]{1,0:T(8,128)(2,1)S(1)}, bf16[64,256]{1,0:T(8,128)(2,1)}, u32[]{:S(2)}) copy-start(bf16[64,256]{1,0:T(8,128)(2,1)} %param.22) | copy-start | bytes 98308
  129.0 14.2 %all-to-all-start.2 = ((bf16[1,64,4,2,128]{4,3,1,0,2:T(2,128)(2,1)}), bf16[1,64,4,2,128]{4,3,1,0,2:T(2,128)(2,1)S(1)}, u32[]{:S(2)}, u32[]{:S(2)}) async-start(bf16[1,64,4,2,128]{4,3,1,0,2:T(2,128)(2,1)} %copy.61), calls=%async_computation.3 | async-start | bytes 262144 | tf_op jit(solution)/shard_map/all_to_all | solution.py:127
  143.1 25.0 %all-to-all-start.3 = ((bf16[1,64,4,2,256]{4,3,1,0,2:T(2,128)(2,1)}), bf16[1,64,4,2,256]{4,3,1,0,2:T(2,128)(2,1)S(1)}, u32[]{:S(2)}, u32[]{:S(2)}) async-start(bf16[1,64,4,2,256]{4,3,1,0,2:T(2,128)(2,1)} %copy.63), calls=%async_computation.4 | async-start | bytes 524288 | tf_op jit(solution)/shard_map/all_to_all | solution.py:130
Sparse Core Ops, SparseCore 0:
  120.1 27.4 reduce-scatter.1
where the time goes:
time: 178 us; the launch traced here: 177 us
  blocking collectives  89 us (50%)
  matrix products  39.5 us (22%)
  starting transfers between devices  16.8 us (9%)
  between operations  13.8 us (8%)
  local copies, waits for them, and re-layouts  7.97 us (4%)
  other arithmetic  5.58 us (3%)
  waiting for transfers between devices  4.78 us (3%)
    psum x1, blocking collectives, local(): inner = lax.psum(partial_inner.astype(jnp.bfloat16), 'tp')  19.8 us
    psum x1, blocking collectives, local(): middle = lax.psum(partial_middle, 'tp').astype(jnp.bfloat16)  19.5 us
    dot_general x3, matrix products, adapted(): jnp.dot(normed, frozen_matrix, preferred_element_type=jnp.float32)  14.8 us
    all_gather x1, blocking collectives, local(): lax.all_gather(input_down_factors, 'rep', axis=1, tiled=True)  12.6 us
    all_gather x1, blocking collectives, local(): lax.all_gather(key_value_up_factors, 'rep', axis=2, tiled=True)  10.9 us
    dot_general x1, matrix products, local(): jnp.dot(context, output_weight_matrix, preferred_element_type=jnp.float32)  9.79 us
    all_gather x1, blocking collectives, local(): lax.all_gather(out_up_rows, 'rep', axis=2, tiled=True)  9.75 us
    dot_general x1, matrix products, attend(): jnp.einsum('bkgd,bkld->bkgl', query, keys.astype(jnp.float32), precision=...  8.5 us
  transfers between devices with their start and end apart: 5, of which 1 were waited for; matrix products, arithmetic and copies ran while one was open for 10% of the time, Pallas kernels for 0%

commit v1 on v0

--- a/solution.py
+++ b/solution.py
@@ -106,7 +106,7 @@
         lax.all_gather(input_down_factors, "rep", axis=1, tiled=True),
         preferred_element_type=jnp.float32,
     )
-    inner = lax.psum(partial_inner.astype(jnp.bfloat16), "tp")
+    inner = jnp.sum(lax.all_gather(partial_inner.astype(jnp.bfloat16), "tp"), axis=0)
     query_up_rows = query_up_factor[None]
     out_down_rows = jnp.swapaxes(output_down_factor, 0, 1)[None]
     out_up_rows = output_up_factor[None]

time: 178 us -> 174 us (0.978)
  blocking collectives: 89 us -> 83.4 us
    psum x1 -> x0, blocking collectives: 19.8 us -> none  [local(): inner = lax.psum(partial_inner.astype(jnp.bfloat16), 'tp')]
    all_gather x0 -> x1, blocking collectives: none -> 14.2 us  [local(): lax.all_gather(partial_inner.astype(jnp.bfloat16), 'tp')]
where the time goes in v1:
time: 174 us; the launch traced here: 173 us
  blocking collectives  83.4 us (48%)
  matrix products  39.5 us (23%)
  starting transfers between devices  18.1 us (10%)
  between operations  13.8 us (8%)
  local copies, waits for them, and re-layouts  7.96 us (5%)
  other arithmetic  5.62 us (3%)
  waiting for transfers between devices  5.04 us (3%)
    psum x1, blocking collectives, local(): middle = lax.psum(partial_middle, 'tp').astype(jnp.bfloat16)  19.5 us
    dot_general x3, matrix products, adapted(): jnp.dot(normed, frozen_matrix, preferred_element_type=jnp.float32)  14.8 us
    all_gather x1, blocking collectives, local(): lax.all_gather(partial_inner.astype(jnp.bfloat16), 'tp')  14.2 us
    all_gather x1, blocking collectives, local(): lax.all_gather(input_down_factors, 'rep', axis=1, tiled=True)  12.6 us
    all_gather x1, blocking collectives, local(): lax.all_gather(key_value_up_factors, 'rep', axis=2, tiled=True)  10.9 us
    all_gather x1, blocking collectives, local(): lax.all_gather(out_up_rows, 'rep', axis=2, tiled=True)  9.81 us
    dot_general x1, matrix products, local(): jnp.dot(context, output_weight_matrix, preferred_element_type=jnp.float32)  9.79 us
    dot_general x1, matrix products, attend(): jnp.einsum('bkgd,bkld->bkgl', query, keys.astype(jnp.float32), precision=...  8.5 us
  transfers between devices with their start and end apart: 5, of which 1 were waited for; matrix products, arithmetic and copies ran while one was open for 10% of the time, Pallas kernels for 0%

profile of v1, /device:TPU:0, one launch (start us, length us, event | category | flops | bytes accessed | tf_op | source)
XLA Modules:
  0.0 173.4 jit_solution(18155087864442590587)
XLA Ops:
  6.5 10.9 %all_gather.25 = bf16[2,64,256]{1,2,0:T(8,128)(2,1)S(1)} all-gather(bf16[2,64,32]{1,2,0:T(8,128)(2,1)} %param.20), channel_id=1, replica_groups=mesh['rep'=8,'tp'=4] {'rep'}, dimensions={2}, use_global_device_ids=true | all-gather | bytes 73728 | tf_op jit(solution)/shard_map/all_gather | solution.py:115
  17.4 0.8 reshape.204
  18.2 4.9 %all-to-all-start.1 = ((bf16[4,2,4096]{2,1,0:T(2,128)(2,1)}), bf16[4,2,4096]{2,1,0:T(2,128)(2,1)S(1)}, u32[]{:S(2)}, u32[]{:S(2)}) async-start(bf16[4,2,4096]{2,1,0:T(2,128)(2,1)} %reshape.204), calls=%async_computation.1 | async-start | bytes 131072 | tf_op jit(solution)/shard_map/all_to_all | solution.py:124
  23.1 0.7 convert_element_type.84
  23.8 1.5 fusion.8
  25.4 1.5 fusion.10
  26.9 0.8 reshape.182
  27.7 3.0 %fusion.2 = f32[64,256]{1,0:T(8,128)S(1)} fusion(bf16[64,8192]{1,0:T(8,128)(2,1)S(1)} %fusion.10, bf16[2,8192,256]{2,1,0:T(8,128)(2,1)} %param.16), kind=kOutput, calls=%fused_computation.3 | convolution fusion | flops 268435456 | bytes 5308416 | tf_op jit(solution)/shard_map/dot_general | solution.py:31
  30.7 3.0 %fusion = f32[64,256]{1,0:T(8,128)S(1)} fusion(bf16[64,8192]{1,0:T(8,128)(2,1)S(1)} %fusion.10, bf16[2,8192,256]{2,1,0:T(8,128)(2,1)} %param.16), kind=kOutput, calls=%fused_computation.1 | convolution fusion | flops 268435456 | bytes 5308416 | tf_op jit(solution)/shard_map/dot_general | solution.py:31
  33.8 1.5 dynamic-slice_reduce_fusion
  35.3 0.1 reshape.200
  35.5 12.6 %all_gather.21 = bf16[3,2048,64]{1,2,0:T(8,128)(2,1)S(1)} all-gather(bf16[3,256,64]{1,2,0:T(8,128)(2,1)S(1)} %copy-done), channel_id=1, replica_groups=mesh['rep'=8,'tp'=4] {'rep'}, dimensions={1}, use_global_device_ids=true | all-gather | bytes 884736 | tf_op jit(solution)/shard_map/all_gather | solution.py:106
  48.0 0.4 fusion.17
  48.5 0.2 multiply_cosine_fusion
  48.8 8.3 %all-gather.1 = bf16[64,1024]{1,0:T(8,128)(2,1)S(1)} all-gather(bf16[64,128]{1,0:T(8,128)(2,1)S(1)} %copy-done.2), channel_id=3, replica_groups=mesh['rep'=8,'tp'=4] {'rep'}, dimensions={1}, use_global_device_ids=true | all-gather | bytes 147456 | tf_op jit(solution)/shard_map/all_gather | solution.py:114
  57.1 0.7 copy.50
  57.9 14.2 %all-gather = bf16[12,64,64]{2,1,0:T(8,128)(2,1)S(1)} all-gather(bf16[3,64,64]{2,1,0:T(8,128)(2,1)S(1)} %fusion.17), channel_id=2, replica_groups=mesh['rep'=8,'tp'=4] {'tp'}, dimensions={0}, use_global_device_ids=true | all-gather | bytes 122880 | tf_op jit(solution)/shard_map/all_gather | solution.py:109
  72.1 4.8 %all-to-all-start = ((bf16[1,64,4,2,128]{4,3,1,0,2:T(2,128)(2,1)}), bf16[1,64,4,2,128]{4,3,1,0,2:T(2,128)(2,1)S(1)}, u32[]{:S(2)}, u32[]{:S(2)}) async-start(bf16[1,64,4,2,128]{4,3,1,0,2:T(2,128)(2,1)} %copy.50), calls=%async_computation | async-start | bytes 262144 | tf_op jit(solution)/shard_map/all_to_all | solution.py:121
  77.0 0.1 reshape.205
  77.2 0.2 fusion.14
  77.4 0.2 fusion.16
  77.5 0.2 subtract_convert_fusion
  77.9 5.0 %all-to-all-done = bf16[1,64,4,2,128]{4,3,1,0,2:T(2,128)(2,1)S(1)} async-done(((bf16[1,64,4,2,128]{4,3,1,0,2:T(2,128)(2,1)}), bf16[1,64,4,2,128]{4,3,1,0,2:T(2,128)(2,1)S(1)}, u32[]{:S(2)}, u32[]{:S(2)}) %all-to-all-start) | async-done | bytes 131104 | tf_op jit(solution)/shard_map/all_to_all | solution.py:121
  82.9 0.2 copy.51
  83.1 0.2 convolution_multiply_fusion.2
  83.3 8.8 %fusion.11 = f32[8,8,8,128]{3,1,2,0:T(8,128)S(1)} fusion(f32[64,1024]{1,0:T(8,128)S(1)} %convolution_multiply_fusion.2, bf16[64,8192]{1,0:T(8,128)(2,1)S(1)} %fusion.10, bf16[8192,1024]{1,0:T(8,128)(2,1)} %param.15), kind=kOutput, calls=%fused_computation.19 | convolution fusion | flops 1073807360 | bytes 18350080 | tf_op jit(solution)/shard_map/dot_general | solution.py:31
  92.2 0.2 multiply_subtract_fusion
  92.4 0.1 pad_maximum_fusion
  92.5 0.4 fusion.18
  93.0 8.5 %select_reduce_fusion = (f32[64,2,4]{2,1,0:T(2,128)S(1)}, f32[64,2,4,128]{3,2,1,0:T(4,128)S(1)}) fusion(pred[64,128]{1,0:T(8,128)(4,1)S(1)} %iota_compare_fusion, f32[64,2,4,128]{3,2,1,0:T(4,128)S(1)} %bitcast.59, bf16[64,2,128,128]{3,2,1,0:T(8,128)(2,1)} %param.23), kind=kOutput, calls=%fused_computation.34 | convolution fusion | flops 100859392 | bytes 4728832 | tf_op jit(solution)/shard_map/bkgd,bkld->bkgl/dot_general | solution.py:40
  101.6 0.1 copy.56
  101.8 0.4 fusion.19
  102.4 0.1 copy.59
  102.6 3.5 %fusion.12 = bf16[64,2,4,128]{3,2,1,0:T(4,128)(2,1)S(1)} fusion(bf16[64,2,128,128]{3,2,1,0:T(8,128)(2,1)} %param.24, f32[64,2,4,128]{3,2,1,0:T(4,128)S(1)} %get-tuple-element.16, f32[64,2,128]{2,1,0:T(2,128)S(1)} %reshape.192, f32[64,2,4]{2,1,0:T(2,128)S(1)} %copy.59, f32[64,2,4]{2,1,0:T(2,128)S(1)} %copy.58, f32[64,2,4]{2,1,0:T(2,128)S(1)} %copy.56, ...), kind=kOutput, calls=%fused_computation.20 | convolution fusion | flops 17235968 | bytes 4667392 | tf_op jit(solution)/shard_map/bkgl,bkld->bkgd/dot_general | solution.py:56
  106.1 9.8 %convolution_convert_fusion = bf16[64,8192]{1,0:T(8,128)(2,1)} fusion(bf16[64,1024]{1,0:T(8,128)(2,1)S(1)} %reshape.189, bf16[1024,8192]{1,0:T(8,128)(2,1)} %param.17), kind=kOutput, calls=%fused_computation | convolution fusion | flops 1074266112 | bytes 17956864 | tf_op jit(solution)/shard_map/dot_general | solution.py:161
  115.9 8.1 %all-gather.2 = bf16[64,1024]{1,0:T(8,128)(2,1)S(1)} all-gather(bf16[64,128]{1,0:T(8,128)(2,1)S(1)} %bitcast.68), channel_id=4, replica_groups=mesh['rep'=8,'tp'=4] {'rep'}, dimensions={1}, use_global_device_ids=true | all-gather | bytes 147456 | tf_op jit(solution)/shard_map/all_gather | solution.py:116
  124.1 0.7 copy.61
  124.9 3.3 %all-to-all-start.2 = ((bf16[1,64,4,2,128]{4,3,1,0,2:T(2,128)(2,1)}), bf16[1,64,4,2,128]{4,3,1,0,2:T(2,128)(2,1)S(1)}, u32[]{:S(2)}, u32[]{:S(2)}) async-start(bf16[1,64,4,2,128]{4,3,1,0,2:T(2,128)(2,1)} %copy.61), calls=%async_computation.3 | async-start | bytes 262144 | tf_op jit(solution)/shard_map/all_to_all | solution.py:127
  128.2 9.8 %all-gather.3 = bf16[64,2048]{1,0:T(8,128)(2,1)S(1)} all-gather(bf16[64,256]{1,0:T(8,128)(2,1)S(1)} %copy-done.1), channel_id=5, replica_groups=mesh['rep'=8,'tp'=4] {'rep'}, dimensions={1}, use_global_device_ids=true | all-gather | bytes 294912 | tf_op jit(solution)/shard_map/all_gather | solution.py:117
  138.0 0.2 reshape.191
  138.2 0.9 copy.63
  139.1 5.0 %all-to-all-start.3 = ((bf16[1,64,4,2,256]{4,3,1,0,2:T(2,128)(2,1)}), bf16[1,64,4,2,256]{4,3,1,0,2:T(2,128)(2,1)S(1)}, u32[]{:S(2)}, u32[]{:S(2)}) async-start(bf16[1,64,4,2,256]{4,3,1,0,2:T(2,128)(2,1)} %copy.63), calls=%async_computation.4 | async-start | bytes 524288 | tf_op jit(solution)/shard_map/all_to_all | solution.py:130
  144.1 0.2 copy.62
  144.4 0.2 fusion.29
  144.5 19.5 %psum.7 = bf16[64,64]{1,0:T(8,128)(2,1)S(1)} all-reduce(f32[64,64]{1,0:T(8,128)S(1)} %fusion.29), channel_id=1, replica_groups=mesh['rep'=8,'tp'=4] {'tp'}, use_global_device_ids=true, to_apply=%region_6.7 | all-reduce | flops 4096 | bytes 24576 | tf_op jit(solution)/shard_map/psum | solution.py:160
  164.1 0.3 copy.64
  164.4 0.2 squeeze_reshape.11
  164.7 1.9 %fusion.7 = bf16[64,2048]{1,0:T(8,128)(2,1)} fusion(bf16[64,2048]{1,0:T(8,128)(2,1)S(1)} %squeeze_reshape.11, bf16[64,2048]{1,0:T(8,128)(2,1)} %reduce-scatter.2.cloned.1.call-done, bf16[64,64]{1,0:T(8,128)(2,1)S(1)} %psum.7), kind=kOutput, calls=%fused_computation.11 | convolution fusion | flops 17301504 | bytes 794624 | tf_op jit(solution)/shard_map/dot_general | solution.py:165
  (41 shorter events, 1.3 us)
Async XLA Ops:
  18.2 53.9 %all-to-all-start.1 = ((bf16[4,2,4096]{2,1,0:T(2,128)(2,1)}), bf16[4,2,4096]{2,1,0:T(2,128)(2,1)S(1)}, u32[]{:S(2)}, u32[]{:S(2)}) async-start(bf16[4,2,4096]{2,1,0:T(2,128)(2,1)} %reshape.204), calls=%async_computation.1 | async-start | bytes 131072 | tf_op jit(solution)/shard_map/all_to_all | solution.py:124
  30.7 4.7 %copy-start = (bf16[3,256,64]{1,2,0:T(8,128)(2,1)S(1)}, bf16[3,256,64]{1,2,0:T(8,128)(2,1)}, u32[]{:S(2)}) copy-start(bf16[3,256,64]{1,2,0:T(8,128)(2,1)} %param.18) | copy-start | bytes 294916
  30.7 17.3 %copy-start.4 = (s32[64]{0:T(128)S(1)}, s32[64]{0:T(128)}, u32[]{:S(2)}) copy-start(s32[64]{0:T(128)} %param.25) | copy-start | bytes 772
  30.7 18.0 %copy-start.2 = (bf16[64,128]{1,0:T(8,128)(2,1)S(1)}, bf16[64,128]{1,0:T(8,128)(2,1)}, u32[]{:S(2)}) copy-start(bf16[64,128]{1,0:T(8,128)(2,1)} %param.19) | copy-start | bytes 49156
  72.1 10.8 %all-to-all-start = ((bf16[1,64,4,2,128]{4,3,1,0,2:T(2,128)(2,1)}), bf16[1,64,4,2,128]{4,3,1,0,2:T(2,128)(2,1)S(1)}, u32[]{:S(2)}, u32[]{:S(2)}) async-start(bf16[1,64,4,2,128]{4,3,1,0,2:T(2,128)(2,1)} %copy.50), calls=%async_computation | async-start | bytes 262144 | tf_op jit(solution)/shard_map/all_to_all | solution.py:121
  77.0 87.7 %reduce-scatter.2.cloned.1.call-start = ((), (), s32[]{:S(2)}) async-start(), calls=%async_computation.5 | async-start | bytes 1310720 | tf_op jit(solution)/shard_map/reduce_scatter | solution.py:162
  106.1 9.8 %copy-start.3 = (bf16[128,64]{0,1:T(8,128)(2,1)S(1)}, bf16[128,64]{0,1:T(8,128)(2,1)}, u32[]{:S(2)}) copy-start(bf16[128,64]{0,1:T(8,128)(2,1)} %param.21) | copy-start | bytes 49156
  106.1 22.1 %copy-start.1 = (bf16[64,256]{1,0:T(8,128)(2,1)S(1)}, bf16[64,256]{1,0:T(8,128)(2,1)}, u32[]{:S(2)}) copy-start(bf16[64,256]{1,0:T(8,128)(2,1)} %param.22) | copy-start | bytes 98308
  124.9 14.2 %all-to-all-start.2 = ((bf16[1,64,4,2,128]{4,3,1,0,2:T(2,128)(2,1)}), bf16[1,64,4,2,128]{4,3,1,0,2:T(2,128)(2,1)S(1)}, u32[]{:S(2)}, u32[]{:S(2)}) async-start(bf16[1,64,4,2,128]{4,3,1,0,2:T(2,128)(2,1)} %copy.61), calls=%async_computation.3 | async-start | bytes 262144 | tf_op jit(solution)/shard_map/all_to_all | solution.py:127
  139.1 25.0 %all-to-all-start.3 = ((bf16[1,64,4,2,256]{4,3,1,0,2:T(2,128)(2,1)}), bf16[1,64,4,2,256]{4,3,1,0,2:T(2,128)(2,1)S(1)}, u32[]{:S(2)}, u32[]{:S(2)}) async-start(bf16[1,64,4,2,256]{4,3,1,0,2:T(2,128)(2,1)} %copy.63), calls=%async_computation.4 | async-start | bytes 524288 | tf_op jit(solution)/shard_map/all_to_all | solution.py:130
Sparse Core Ops, SparseCore 0:
  116.1 27.4 reduce-scatter.1
